TPU v7x, 32 devices: a whole 2x2x4 slice. The times are simulated.
32 devices in a mesh: blk: 4 (over z), pts: 8 (over y, x, core).
Axes of the slice: x: 2, y: 2, z: 4, core: 2. Of those that a mesh axis runs over, the one named last changes fastest.
Arguments:
- signal: bfloat16 [67584, 2048], P('blk', 'pts'), may hold values from -6 to 6
- offsets: int32 [128], P('blk'), may hold values from 0 to 15872
- kept: int32 [16], replicated, may hold values from 0 to 512
- weights: float32 [2048], P('pts'), may hold values from 0.2 to 5
Outputs:
- gram: float32 [16, 2, 128, 128], P('pts', None, 'blk')
Inputs may be any that keep to these rules, and one draw needn't show every extreme that they name: `kept`: indices may repeat.
All inputs are finite; a program needn't handle non-finite values.
Results may differ from a plain program's by a relative error of at most 0.0022.
Values may be sent and summed in bfloat16 or wider, within the bound.
A program may use at most 128 MiB of HBM per device.

v0:
```python
import math

import jax
import jax.numpy as jnp
from jax import lax
from jax.sharding import PartitionSpec as P

NFFT = 1024


def spectral_table(kept, length):
    times = jnp.arange(length, dtype=jnp.int32)
    window = 0.5 - 0.5 * jnp.cos(times.astype(jnp.float32) * (2.0 * math.pi / length))
    norm = 1.0 / jnp.sqrt(jnp.sum(window * window))
    phase_index = times[:, None] * kept[None, :] % length
    phase = phase_index.astype(jnp.float32) * (2.0 * math.pi / length)
    cosine = (norm * window)[:, None] * jnp.cos(phase)
    sine = -(norm * window)[:, None] * jnp.sin(phase)
    return jnp.concatenate([cosine, sine], axis=1).astype(jnp.bfloat16)


def gram_terms(owned, piece):
    own_re = owned[:, 0]
    own_im = owned[:, 1]
    far_re = piece[:, 0]
    far_im = piece[:, 1]
    gram_re = jnp.einsum("bfp,nfp->fbn", own_re, far_re, preferred_element_type=jnp.float32)
    gram_re = gram_re + jnp.einsum(
        "bfp,nfp->fbn", own_im, far_im, preferred_element_type=jnp.float32
    )
    gram_im = jnp.einsum("bfp,nfp->fbn", own_re, far_im, preferred_element_type=jnp.float32)
    gram_im = gram_im - jnp.einsum(
        "bfp,nfp->fbn", own_im, far_re, preferred_element_type=jnp.float32
    )
    return jnp.stack([gram_re, gram_im], axis=1)


def on_device(signal, offsets, kept, weights):
    blocks_here = offsets.shape[0]
    points_here = signal.shape[1]
    freq_all = kept.shape[0]
    total_points = points_here * lax.axis_size("pts")
    table = spectral_table(kept, NFFT)

    def take_block(start):
        return lax.dynamic_slice(signal, (start, jnp.int32(0)), (NFFT, points_here))

    stacked = jax.vmap(take_block)(offsets)
    values = jnp.einsum("tk,btp->bkp", table, stacked, preferred_element_type=jnp.float32)
    scale = jnp.sqrt(weights / total_points)
    spectra = (
        (values * scale[None, None, :])
        .astype(jnp.bfloat16)
        .reshape(blocks_here, 2, freq_all, points_here)
    )
    moved = lax.all_to_all(spectra, "pts", split_axis=2, concat_axis=3, tiled=True)
    return gram_terms(moved, lax.all_gather(moved, "blk", axis=0, tiled=True))


def solution(mesh):
    placed = (P("blk", "pts"), P("blk"), P(), P("pts"))
    return jax.shard_map(
        on_device,
        mesh=mesh,
        in_specs=placed,
        out_specs=P("pts", None, "blk", None),
        check_vma=False,
    )
```

profile of v0, /device:TPU:0, one launch (start us, length us, event | category | flops | bytes accessed | tf_op | source)
XLA Modules:
  0.0 197.6 jit_solution(337852461670066417)
XLA Ops:
  7.9 102.3 %while.1 = (s32[]{:T(128)}, bf16[16896,256]{1,0:T(8,128)(2,1)}, s32[32,2]{0,1:T(2,128)S(1)}, bf16[32,1024,256]{2,1,0:T(8,128)(2,1)}, s32[]{:T(128)}) while((s32[]{:T(128)}, bf16[16896,256]{1,0:T(8,128)(2,1)}, s32[32,2]{0,1:T(2,128)S(1)}, bf16[32,1024,256]{2,1,0:T(8,128)(2,1)}, s32[]{:T(128)}) %tuple.18), condition=%wide.while_cond, body=%wide.while_body.sunk | while | flops 2 | bytes 1049189 | solution.py:46
  14.8 2.6 %bitcast_dynamic-update-slice_fusion.2 = bf16[32,1024,256]{2,1,0:T(8,128)(2,1)} fusion(bf16[32,1024,256]{2,1,0:T(8,128)(2,1)} %get-tuple-element.58, s32[]{:T(128)S(6)} %copy.15, bf16[16896,256]{1,0:T(8,128)(2,1)} %get-tuple-element.61, s32[]{:T(128)} %bitcast.43), kind=kLoop, calls=%fused_computation.clone.1 | loop fusion | bytes 1049092 | tf_op jit(solution)/shard_map/vmap()/gather
  21.2 2.6 %bitcast_dynamic-update-slice_fusion.2 = bf16[32,1024,256]{2,1,0:T(8,128)(2,1)} fusion(bf16[32,1024,256]{2,1,0:T(8,128)(2,1)} %get-tuple-element.58, s32[]{:T(128)S(6)} %copy.15, bf16[16896,256]{1,0:T(8,128)(2,1)} %get-tuple-element.61, s32[]{:T(128)} %bitcast.43), kind=kLoop, calls=%fused_computation.clone.1 | loop fusion | bytes 1049092 | tf_op jit(solution)/shard_map/vmap()/gather
  24.4 2.6 %bitcast_dynamic-update-slice_fusion.2 = bf16[32,1024,256]{2,1,0:T(8,128)(2,1)} fusion(bf16[32,1024,256]{2,1,0:T(8,128)(2,1)} %get-tuple-element.58, s32[]{:T(128)S(6)} %copy.15, bf16[16896,256]{1,0:T(8,128)(2,1)} %get-tuple-element.61, s32[]{:T(128)} %bitcast.43), kind=kLoop, calls=%fused_computation.clone.1 | loop fusion | bytes 1049092 | tf_op jit(solution)/shard_map/vmap()/gather
  34.0 2.6 %bitcast_dynamic-update-slice_fusion.2 = bf16[32,1024,256]{2,1,0:T(8,128)(2,1)} fusion(bf16[32,1024,256]{2,1,0:T(8,128)(2,1)} %get-tuple-element.58, s32[]{:T(128)S(6)} %copy.15, bf16[16896,256]{1,0:T(8,128)(2,1)} %get-tuple-element.61, s32[]{:T(128)} %bitcast.43), kind=kLoop, calls=%fused_computation.clone.1 | loop fusion | bytes 1049092 | tf_op jit(solution)/shard_map/vmap()/gather
  37.2 2.6 %bitcast_dynamic-update-slice_fusion.2 = bf16[32,1024,256]{2,1,0:T(8,128)(2,1)} fusion(bf16[32,1024,256]{2,1,0:T(8,128)(2,1)} %get-tuple-element.58, s32[]{:T(128)S(6)} %copy.15, bf16[16896,256]{1,0:T(8,128)(2,1)} %get-tuple-element.61, s32[]{:T(128)} %bitcast.43), kind=kLoop, calls=%fused_computation.clone.1 | loop fusion | bytes 1049092 | tf_op jit(solution)/shard_map/vmap()/gather
  40.4 2.6 %bitcast_dynamic-update-slice_fusion.2 = bf16[32,1024,256]{2,1,0:T(8,128)(2,1)} fusion(bf16[32,1024,256]{2,1,0:T(8,128)(2,1)} %get-tuple-element.58, s32[]{:T(128)S(6)} %copy.15, bf16[16896,256]{1,0:T(8,128)(2,1)} %get-tuple-element.61, s32[]{:T(128)} %bitcast.43), kind=kLoop, calls=%fused_computation.clone.1 | loop fusion | bytes 1049092 | tf_op jit(solution)/shard_map/vmap()/gather
  46.8 2.6 %bitcast_dynamic-update-slice_fusion.2 = bf16[32,1024,256]{2,1,0:T(8,128)(2,1)} fusion(bf16[32,1024,256]{2,1,0:T(8,128)(2,1)} %get-tuple-element.58, s32[]{:T(128)S(6)} %copy.15, bf16[16896,256]{1,0:T(8,128)(2,1)} %get-tuple-element.61, s32[]{:T(128)} %bitcast.43), kind=kLoop, calls=%fused_computation.clone.1 | loop fusion | bytes 1049092 | tf_op jit(solution)/shard_map/vmap()/gather
  50.0 2.6 %bitcast_dynamic-update-slice_fusion.2 = bf16[32,1024,256]{2,1,0:T(8,128)(2,1)} fusion(bf16[32,1024,256]{2,1,0:T(8,128)(2,1)} %get-tuple-element.58, s32[]{:T(128)S(6)} %copy.15, bf16[16896,256]{1,0:T(8,128)(2,1)} %get-tuple-element.61, s32[]{:T(128)} %bitcast.43), kind=kLoop, calls=%fused_computation.clone.1 | loop fusion | bytes 1049092 | tf_op jit(solution)/shard_map/vmap()/gather
  56.3 2.6 %bitcast_dynamic-update-slice_fusion.2 = bf16[32,1024,256]{2,1,0:T(8,128)(2,1)} fusion(bf16[32,1024,256]{2,1,0:T(8,128)(2,1)} %get-tuple-element.58, s32[]{:T(128)S(6)} %copy.15, bf16[16896,256]{1,0:T(8,128)(2,1)} %get-tuple-element.61, s32[]{:T(128)} %bitcast.43), kind=kLoop, calls=%fused_computation.clone.1 | loop fusion | bytes 1049092 | tf_op jit(solution)/shard_map/vmap()/gather
  59.6 2.6 %bitcast_dynamic-update-slice_fusion.2 = bf16[32,1024,256]{2,1,0:T(8,128)(2,1)} fusion(bf16[32,1024,256]{2,1,0:T(8,128)(2,1)} %get-tuple-element.58, s32[]{:T(128)S(6)} %copy.15, bf16[16896,256]{1,0:T(8,128)(2,1)} %get-tuple-element.61, s32[]{:T(128)} %bitcast.43), kind=kLoop, calls=%fused_computation.clone.1 | loop fusion | bytes 1049092 | tf_op jit(solution)/shard_map/vmap()/gather
  62.8 2.6 %bitcast_dynamic-update-slice_fusion.2 = bf16[32,1024,256]{2,1,0:T(8,128)(2,1)} fusion(bf16[32,1024,256]{2,1,0:T(8,128)(2,1)} %get-tuple-element.58, s32[]{:T(128)S(6)} %copy.15, bf16[16896,256]{1,0:T(8,128)(2,1)} %get-tuple-element.61, s32[]{:T(128)} %bitcast.43), kind=kLoop, calls=%fused_computation.clone.1 | loop fusion | bytes 1049092 | tf_op jit(solution)/shard_map/vmap()/gather
  72.4 2.6 %bitcast_dynamic-update-slice_fusion.2 = bf16[32,1024,256]{2,1,0:T(8,128)(2,1)} fusion(bf16[32,1024,256]{2,1,0:T(8,128)(2,1)} %get-tuple-element.58, s32[]{:T(128)S(6)} %copy.15, bf16[16896,256]{1,0:T(8,128)(2,1)} %get-tuple-element.61, s32[]{:T(128)} %bitcast.43), kind=kLoop, calls=%fused_computation.clone.1 | loop fusion | bytes 1049092 | tf_op jit(solution)/shard_map/vmap()/gather
  75.6 2.6 %bitcast_dynamic-update-slice_fusion.2 = bf16[32,1024,256]{2,1,0:T(8,128)(2,1)} fusion(bf16[32,1024,256]{2,1,0:T(8,128)(2,1)} %get-tuple-element.58, s32[]{:T(128)S(6)} %copy.15, bf16[16896,256]{1,0:T(8,128)(2,1)} %get-tuple-element.61, s32[]{:T(128)} %bitcast.43), kind=kLoop, calls=%fused_computation.clone.1 | loop fusion | bytes 1049092 | tf_op jit(solution)/shard_map/vmap()/gather
  82.0 2.6 %bitcast_dynamic-update-slice_fusion.2 = bf16[32,1024,256]{2,1,0:T(8,128)(2,1)} fusion(bf16[32,1024,256]{2,1,0:T(8,128)(2,1)} %get-tuple-element.58, s32[]{:T(128)S(6)} %copy.15, bf16[16896,256]{1,0:T(8,128)(2,1)} %get-tuple-element.61, s32[]{:T(128)} %bitcast.43), kind=kLoop, calls=%fused_computation.clone.1 | loop fusion | bytes 1049092 | tf_op jit(solution)/shard_map/vmap()/gather
  85.1 2.6 %bitcast_dynamic-update-slice_fusion.2 = bf16[32,1024,256]{2,1,0:T(8,128)(2,1)} fusion(bf16[32,1024,256]{2,1,0:T(8,128)(2,1)} %get-tuple-element.58, s32[]{:T(128)S(6)} %copy.15, bf16[16896,256]{1,0:T(8,128)(2,1)} %get-tuple-element.61, s32[]{:T(128)} %bitcast.43), kind=kLoop, calls=%fused_computation.clone.1 | loop fusion | bytes 1049092 | tf_op jit(solution)/shard_map/vmap()/gather
  88.4 2.6 %bitcast_dynamic-update-slice_fusion.2 = bf16[32,1024,256]{2,1,0:T(8,128)(2,1)} fusion(bf16[32,1024,256]{2,1,0:T(8,128)(2,1)} %get-tuple-element.58, s32[]{:T(128)S(6)} %copy.15, bf16[16896,256]{1,0:T(8,128)(2,1)} %get-tuple-element.61, s32[]{:T(128)} %bitcast.43), kind=kLoop, calls=%fused_computation.clone.1 | loop fusion | bytes 1049092 | tf_op jit(solution)/shard_map/vmap()/gather
  97.9 2.6 %bitcast_dynamic-update-slice_fusion.2 = bf16[32,1024,256]{2,1,0:T(8,128)(2,1)} fusion(bf16[32,1024,256]{2,1,0:T(8,128)(2,1)} %get-tuple-element.58, s32[]{:T(128)S(6)} %copy.15, bf16[16896,256]{1,0:T(8,128)(2,1)} %get-tuple-element.61, s32[]{:T(128)} %bitcast.43), kind=kLoop, calls=%fused_computation.clone.1 | loop fusion | bytes 1049092 | tf_op jit(solution)/shard_map/vmap()/gather
  101.1 2.6 %bitcast_dynamic-update-slice_fusion.2 = bf16[32,1024,256]{2,1,0:T(8,128)(2,1)} fusion(bf16[32,1024,256]{2,1,0:T(8,128)(2,1)} %get-tuple-element.58, s32[]{:T(128)S(6)} %copy.15, bf16[16896,256]{1,0:T(8,128)(2,1)} %get-tuple-element.61, s32[]{:T(128)} %bitcast.43), kind=kLoop, calls=%fused_computation.clone.1 | loop fusion | bytes 1049092 | tf_op jit(solution)/shard_map/vmap()/gather
  104.3 2.6 %bitcast_dynamic-update-slice_fusion.2 = bf16[32,1024,256]{2,1,0:T(8,128)(2,1)} fusion(bf16[32,1024,256]{2,1,0:T(8,128)(2,1)} %get-tuple-element.58, s32[]{:T(128)S(6)} %copy.15, bf16[16896,256]{1,0:T(8,128)(2,1)} %get-tuple-element.61, s32[]{:T(128)} %bitcast.43), kind=kLoop, calls=%fused_computation.clone.1 | loop fusion | bytes 1049092 | tf_op jit(solution)/shard_map/vmap()/gather
  107.5 2.6 %bitcast_dynamic-update-slice_fusion.2 = bf16[32,1024,256]{2,1,0:T(8,128)(2,1)} fusion(bf16[32,1024,256]{2,1,0:T(8,128)(2,1)} %get-tuple-element.58, s32[]{:T(128)S(6)} %copy.15, bf16[16896,256]{1,0:T(8,128)(2,1)} %get-tuple-element.61, s32[]{:T(128)} %bitcast.43), kind=kLoop, calls=%fused_computation.clone.1 | loop fusion | bytes 1049092 | tf_op jit(solution)/shard_map/vmap()/gather
  112.5 8.7 %fusion = bf16[32,256,32]{1,2,0:T(8,128)(2,1)S(1)} fusion(bf16[32,1024,256]{2,1,0:T(8,128)(2,1)} %get-tuple-element.12, f32[256]{0:T(256)S(1)} %multiply_sqrt_fusion, bf16[1024,16]{0,1:T(8,128)(2,1)S(1)} %get-tuple-element.22, bf16[1024,16]{0,1:T(8,128)(2,1)S(1)} %get-tuple-element.21), kind=kOutput, calls=%fused_computation.3 | convolution fusion | flops 537526272 | bytes 17368064 | tf_op jit(solution)/shard_map/tk,btp->bkp/dot_general | solution.py:49
  121.8 14.7 %all_to_all.18 = bf16[32,2,16,256]{3,1,0,2:T(2,128)(2,1)S(1)} all-to-all(bf16[32,2,16,256]{3,1,0,2:T(2,128)(2,1)S(1)} %copy.7), channel_id=1, replica_groups=mesh['blk'=4,'pts'=8] {'pts'}, dimensions={2} | all-to-all | bytes 1048576 | tf_op jit(solution)/shard_map/all_to_all | solution.py:56
  137.8 45.2 %all-gather.2.cloned.1.call-done = bf16[128,2,2,2048]{3,0,2,1:T(8,128)(2,1)} async-done(((bf16[32,2,2,2048]{3,0,2,1:T(8,128)(2,1)}), bf16[128,2,2,2048]{3,0,2,1:T(8,128)(2,1)}) %all-gather.2.cloned.1.call-update) | async-done | bytes 2097168 | tf_op jit(solution)/shard_map/all_gather | solution.py:57
  (94 shorter events, 63.0 us)
Async XLA Ops:
  6.5 176.5 %all-gather.2.cloned.1.call-start = ((), (), s32[]{:S(2)}) async-start(), calls=%async_computation.1 | async-start | bytes 2621440 | tf_op jit(solution)/shard_map/all_gather | solution.py:57
Sparse Core Ops, SparseCore 0:
  138.0 45.0 all-gather.1
where the time goes:
time: 200 us; the launch traced here: 198 us
  local copies, waits for them, and re-layouts  105 us (52%)
  waiting for transfers between devices  45.2 us (23%)
  matrix products  15.8 us (8%)
  blocking collectives  14.7 us (7%)
  between operations  14.1 us (7%)
  other arithmetic  3.06 us (2%)
    gather x96, local copies, waits for them, and re-layouts  102 us
    all_gather x1, waiting for transfers between devices, on_device(): return gram_terms(moved, lax.all_gather(moved, 'blk', axis=0, tiled=True))  45.2 us
    all_to_all x1, blocking collectives, on_device(): lax.all_to_all(spectra, 'pts', split_axis=2, concat_axis=3, tiled=True)  14.7 us
    dot_general x1, matrix products, on_device(): jnp.einsum('tk,btp->bkp', table, stacked, preferred_element_type=jnp.floa...  8.74 us
  transfers between devices with their start and end apart: 1, of which 1 were waited for; matrix products, arithmetic and copies ran while one was open for 0% of the time, Pallas kernels for 0%

commit v1 on v0

v1 whole, which is shorter than its diff:
```python
import functools
import math

import jax
import jax.numpy as jnp
from jax import lax
from jax.experimental import pallas as pl
from jax.experimental.pallas import tpu as pltpu
from jax.sharding import PartitionSpec as P

NFFT = 1024
ALIGN = 16
LANES = 128
SPAN = NFFT + LANES
PIECES = 8
UNROLL = 8
MESH = pl.DeviceIdType.MESH


def fill_tables(kept_ref, table_ref):
    kept_all = kept_ref.shape[0]
    shape = (kept_all, NFFT)
    times = lax.broadcasted_iota(jnp.int32, shape, 1)
    row = lax.broadcasted_iota(jnp.int32, shape, 0)
    kept = jnp.zeros(shape, jnp.int32)
    for k in range(kept_all):
        kept = jnp.where(row == k, kept_ref[k], kept)
    step = 2.0 * math.pi / NFFT
    line = lax.broadcasted_iota(jnp.int32, (8, NFFT), 1)
    window = 0.5 - 0.5 * jnp.cos(line.astype(jnp.float32) * step)
    norm = 1.0 / jnp.sqrt(jnp.sum(window[:1] * window[:1], axis=1, keepdims=True))
    gain = norm * window[:1]
    phase = ((times * kept) & (NFFT - 1)).astype(jnp.float32) * step
    tail = jnp.zeros((2 * kept_all, SPAN - NFFT), jnp.float32)
    base = jnp.concatenate([gain * jnp.cos(phase), -gain * jnp.sin(phase)], axis=0)
    base = jnp.concatenate([base, tail], axis=1)
    for shift in range(ALIGN):
        moved = base if shift == 0 else pltpu.roll(base, shift, 1)
        table_ref[shift] = moved.astype(jnp.bfloat16)


def spectra_kernel(
    n_pts,
    signal_ref,
    offsets_ref,
    kept_ref,
    weights_ref,
    spec,
    held,
    table_ref,
    low,
    high,
    load_sem,
):
    seg, points = signal_ref.shape
    blocks = offsets_ref.shape[0]
    freq_all = kept_ref.shape[0]

    loads = []
    rows = seg // PIECES
    for piece in range(PIECES):
        copy = pltpu.make_async_copy(
            signal_ref.at[pl.ds(piece * rows, rows)],
            held.at[pl.ds(piece * rows, rows)],
            load_sem.at[piece],
        )
        copy.start()
        loads.append(copy)

    held[pl.ds(seg, LANES), :] = jnp.zeros((LANES, points), held.dtype)
    fill_tables(kept_ref, table_ref)
    for copy in loads:
        copy.wait()

    def some_blocks(turn, _):
        for inner in range(UNROLL):
            block = turn * UNROLL + inner
            start = offsets_ref[block]
            shift = start & (ALIGN - 1)
            rows_at = pl.multiple_of(start - shift, ALIGN)
            values = jnp.dot(
                table_ref[shift],
                held[pl.ds(rows_at, SPAN), :],
                preferred_element_type=jnp.float32,
            )
            low[pl.ds(block, 2 * freq_all, stride=blocks), :] = values[:, :LANES]
            high[pl.ds(block, 2 * freq_all, stride=blocks), :] = values[:, LANES:]
        return 0

    lax.fori_loop(0, blocks // UNROLL, some_blocks, 0)

    scale = jnp.sqrt(weights_ref[...] / (points * n_pts))

    for c in range(2):
        for k in range(freq_all):
            at = pl.ds((c * freq_all + k) * blocks, blocks)
            both = jnp.concatenate([low[at, :], high[at, :]], axis=1)
            spec[c, k] = (both * scale).astype(jnp.bfloat16)


def gram_kernel(
    n_blk,
    n_pts,
    spec,
    out_ref,
    got,
    gram,
    part,
    far,
    send_sem,
    recv_sem,
    send2_sem,
    recv2_sem,
):
    freq_all, blocks, points = spec.shape[1:]
    freqs = freq_all // n_pts
    groups = n_pts // n_blk
    mine = lax.axis_index("blk")
    col = lax.axis_index("pts")

    def target(step):
        dest = lax.rem(col + step, n_pts)
        return lax.rem(col + dest, n_blk), dest

    def source(group, step):
        origin = lax.rem(mine + n_blk - lax.rem(col, n_blk), n_blk) + group * n_blk
        return lax.rem(mine + step, n_blk), origin

    barrier = pltpu.get_barrier_semaphore()

    def greet(where):
        pl.semaphore_signal(barrier, inc=1, device_id=where, device_id_type=MESH)

    for step in range(n_pts):
        greet(target(step))
    for group in range(groups):
        for step in range(n_blk):
            greet(source(group, step))
    for step in range(1, n_blk):
        where = (lax.rem(mine + step, n_blk), col)
        pl.semaphore_signal(barrier, inc=1, device_id=where, device_id_type=MESH)

    pl.semaphore_wait(barrier, 2 * n_pts + n_blk - 1)

    slot = lax.div(col, n_blk)

    def send(step):
        where = target(step)
        return pltpu.make_async_remote_copy(
            src_ref=spec.at[:, pl.ds(where[1] * freqs, freqs)],
            dst_ref=got.at[slot, :, :, mine],
            send_sem=send_sem.at[step],
            recv_sem=recv_sem.at[slot, mine],
            device_id=where,
            device_id_type=MESH,
        )

    own = lax.rem(2 * col, n_blk) == mine

    @pl.when(own)
    def _():
        pltpu.make_async_copy(
            spec.at[:, pl.ds(col * freqs, freqs)],
            got.at[slot, :, :, mine],
            recv_sem.at[slot, mine],
        ).start()

    @pl.when(jnp.logical_not(own))
    def _():
        send(0).start()

    for step in range(1, n_pts):
        send(step).start()

    for group in range(groups):
        for z in range(n_blk):
            pltpu.make_async_copy(
                spec.at[:, pl.ds(0, freqs)], got.at[group, :, :, z], recv_sem.at[group, z]
            ).wait()

    whole = n_blk * blocks
    for f in range(freqs):
        total = jnp.zeros((2 * whole, 2 * whole), jnp.float32)
        for group in range(groups):
            x = jnp.concatenate(
                [
                    got[group, 0, f].reshape(whole, points),
                    got[group, 1, f].reshape(whole, points),
                ],
                axis=0,
            )
            total = total + lax.dot_general(
                x, x, (((1,), (1,)), ((), ())), preferred_element_type=jnp.float32
            )
        real = total[:whole, :whole] + total[whole:, whole:]
        imag = total[:whole, whole:] - total[whole:, :whole]
        for c, value in ((0, real), (1, imag)):
            for z in range(n_blk):
                rows_z = value[z * blocks : (z + 1) * blocks]
                gram[z, f, c] = rows_z
                part[z, f, c] = rows_z.astype(jnp.bfloat16)

    def give(step):
        to = lax.rem(mine + step, n_blk)
        return pltpu.make_async_remote_copy(
            src_ref=part.at[to],
            dst_ref=far.at[step - 1],
            send_sem=send2_sem.at[step - 1],
            recv_sem=recv2_sem.at[step - 1],
            device_id=(to, col),
            device_id_type=MESH,
        )

    for step in range(1, n_blk):
        give(step).start()
    result = gram[mine]
    for step in range(1, n_blk):
        give(step).wait_recv()
        result = result + far[step - 1].astype(jnp.float32)
    out_ref[...] = result

    for step in range(1, n_blk):
        give(step).wait_send()

    @pl.when(jnp.logical_not(own))
    def _():
        send(0).wait_send()

    for step in range(1, n_pts):
        send(step).wait_send()


def on_device(n_blk, n_pts, signal, offsets, kept, weights):
    seg, points = signal.shape
    blocks = offsets.shape[0]
    freq_all = kept.shape[0]
    freqs = freq_all // n_pts
    groups = n_pts // n_blk
    whole = n_blk * blocks
    vmem = pl.BlockSpec(memory_space=pltpu.VMEM)
    smem = pl.BlockSpec(memory_space=pltpu.SMEM)
    spec = pl.pallas_call(
        functools.partial(spectra_kernel, n_pts),
        out_shape=jax.ShapeDtypeStruct((2, freq_all, blocks, points), jnp.bfloat16),
        in_specs=[pl.BlockSpec(memory_space=pl.ANY), smem, smem, vmem],
        out_specs=vmem,
        scratch_shapes=[
            pltpu.VMEM((seg + LANES, points), jnp.bfloat16),
            pltpu.VMEM((ALIGN, 2 * freq_all, SPAN), jnp.bfloat16),
            pltpu.VMEM((2 * freq_all * blocks, LANES), jnp.float32),
            pltpu.VMEM((2 * freq_all * blocks, LANES), jnp.float32),
            pltpu.SemaphoreType.DMA((PIECES,)),
        ],
        compiler_params=pltpu.CompilerParams(vmem_limit_bytes=48 * 1024 * 1024),
    )(signal, offsets, kept, weights.reshape(1, points))
    return pl.pallas_call(
        functools.partial(gram_kernel, n_blk, n_pts),
        out_shape=jax.ShapeDtypeStruct((freqs, 2, blocks, whole), jnp.float32),
        in_specs=[vmem],
        out_specs=vmem,
        scratch_shapes=[
            pltpu.VMEM((groups, 2, freqs, n_blk, blocks, points), jnp.bfloat16),
            pltpu.VMEM((n_blk, freqs, 2, blocks, whole), jnp.float32),
            pltpu.VMEM((n_blk, freqs, 2, blocks, whole), jnp.bfloat16),
            pltpu.VMEM((n_blk - 1, freqs, 2, blocks, whole), jnp.bfloat16),
            pltpu.SemaphoreType.DMA((n_pts,)),
            pltpu.SemaphoreType.DMA((groups, n_blk)),
            pltpu.SemaphoreType.DMA((n_blk - 1,)),
            pltpu.SemaphoreType.DMA((n_blk - 1,)),
        ],
        compiler_params=pltpu.CompilerParams(
            collective_id=0, has_side_effects=True, vmem_limit_bytes=32 * 1024 * 1024
        ),
    )(spec)


def solution(mesh):
    placed = (P("blk", "pts"), P("blk"), P(), P("pts"))
    return jax.shard_map(
        functools.partial(on_device, mesh.shape["blk"], mesh.shape["pts"]),
        mesh=mesh,
        in_specs=placed,
        out_specs=P("pts", None, "blk", None),
        check_vma=False,
    )
```

time: 200 us -> 36.2 us (0.18); the launches traced: 198 us -> 36.1 us
  local copies, waits for them, and re-layouts: 105 us -> 2.62 us
  waiting for transfers between devices: 45.2 us -> 0 us
  Pallas kernels: 0 us -> 33.4 us
  matrix products: 15.8 us -> 0 us
  blocking collectives: 14.7 us -> 0 us
  between operations: 14.1 us -> 0.02 us
  other arithmetic: 3.06 us -> 0 us
    gather x96 -> x0, local copies, waits for them, and re-layouts: 102 us -> none
    all_gather x1 -> x0, waiting for transfers between devices: 45.2 us -> none  [on_device(): return gram_terms(moved, lax.all_gather(moved, 'blk', axis=0, tiled=True))]
    pallas_call x0 -> x2, Pallas kernels: none -> 33.4 us  [the longest x1 25.1 us: on_device(): pl.pallas_call(functools.partial(gram_kernel, n_blk, n_pts), out_shape=ja...]
    dot_general x5 -> x0, matrix products: 15.8 us -> none  [the longest x1 8.74 us: on_device(): jnp.einsum('tk,btp->bkp', table, stacked, preferred_element_type=jnp.floa...]
    all_to_all x1 -> x0, blocking collectives: 14.7 us -> none  [on_device(): lax.all_to_all(spectra, 'pts', split_axis=2, concat_axis=3, tiled=True)]
    unnamed x0 -> x7, local copies, waits for them, and re-layouts: none -> 2.62 us
  transfers between devices with their start and end apart: 1 -> 0, of which waited for: 1 -> 0; matrix products, arithmetic and copies ran while one was open for 0% -> 0% of each run, Pallas kernels for 0% -> 0%
where the time goes in v1:
time: 36.2 us; the launch traced here: 36.1 us
  Pallas kernels  33.4 us (92%)
  local copies, waits for them, and re-layouts  2.62 us (7%)
    pallas_call x1, Pallas kernels, on_device(): pl.pallas_call(functools.partial(gram_kernel, n_blk, n_pts), out_shape=ja...  25.1 us
    pallas_call x1, Pallas kernels, on_device(): pl.pallas_call(functools.partial(spectra_kernel, n_pts), out_shape=jax.Sh...  8.38 us
    unnamed x7, local copies, waits for them, and re-layouts  2.62 us

profile of v1, /device:TPU:0, one launch (start us, length us, event | category | flops | bytes accessed | tf_op | source)
XLA Modules:
  0.0 36.1 jit_solution(7719966966911021496)
XLA Ops:
  0.0 0.0 copy-start
  0.0 0.7 %copy-done = f32[256]{0:T(256)S(1)} copy-done((f32[256]{0:T(256)S(1)}, f32[256]{0:T(256)}, u32[]{:S(2)}) %copy-start) | copy-done | bytes 1048
  0.7 0.0 copy-start.1
  0.7 0.7 %copy-done.1 = s32[32]{0:T(128)S(1)} copy-done((s32[32]{0:T(128)S(1)}, s32[32]{0:T(128)}, u32[]{:S(2)}) %copy-start.1) | copy-done | bytes 152
  1.3 0.0 copy-start.2
  1.3 0.7 %copy-done.2 = s32[16]{0:T(128)S(1)} copy-done((s32[16]{0:T(128)S(1)}, s32[16]{0:T(128)}, u32[]{:S(2)}) %copy-start.2) | copy-done | bytes 88
  2.0 8.4 %shard_map.46.spec = bf16[2,16,32,256]{3,2,1,0:T(8,128)(2,1)S(1)} custom-call(bf16[16896,256]{1,0:T(8,128)(2,1)} %signal_ref.1, s32[32]{0:T(128)S(1)} %copy-done.1, s32[16]{0:T(128)S(1)} %copy-done.2, f32[1,256]{1,0:T(1,128)S(1)} %bitcast.1), custom_call_target="tpu_custom_call" | custom-call | tf_op jit(solution)/shard_map/pallas_call | solution.py:242
  10.4 25.1 %shard_map.47 = f32[2,2,32,128]{3,2,1,0:T(8,128)S(1)} custom-call(bf16[2,16,32,256]{3,2,1,0:T(8,128)(2,1)S(1)} %shard_map.46.spec), custom_call_target="tpu_custom_call" | custom-call | tf_op jit(solution)/shard_map/pallas_call | solution.py:256
  35.4 0.6 %copy.6 = f32[2,2,32,128]{3,2,1,0:T(8,128)} copy(f32[2,2,32,128]{3,2,1,0:T(8,128)S(1)} %shard_map.47) | data formatting | bytes 131072
Async XLA Ops:
  0.0 0.7 %copy-start = (f32[256]{0:T(256)S(1)}, f32[256]{0:T(256)}, u32[]{:S(2)}) copy-start(f32[256]{0:T(256)} %param.7) | copy-start | bytes 3076
  0.7 0.7 %copy-start.1 = (s32[32]{0:T(128)S(1)}, s32[32]{0:T(128)}, u32[]{:S(2)}) copy-start(s32[32]{0:T(128)} %offsets_ref.1) | copy-start | bytes 388
  1.3 0.7 %copy-start.2 = (s32[16]{0:T(128)S(1)}, s32[16]{0:T(128)}, u32[]{:S(2)}) copy-start(s32[16]{0:T(128)} %kept_ref.1) | copy-start | bytes 196
